TPU v7x, 256 devices: a whole 4x4x8 slice. The times are simulated.
256 devices in a mesh: ens: 4 (over x), slab: 64 (over y, z, core).
Axes of the slice: x: 4, y: 4, z: 8, core: 2. Of those that a mesh axis runs over, the one named last changes fastest.
Arguments:
- velocity: float32 [4, 3, 8, 2048, 1024], P('ens', None, None, 'slab'), may hold values from -6 to 6
- cutoffs: int32 [4, 2, 8], P('ens'), may hold values from 128 to 511, as said below
- plane_index: int32 [4], P('ens'), may hold values from 0 to 2047
- boundary_index: int32 [4], P('ens'), may hold values from 0 to 2047
Outputs:
- blended: float32 [4, 3, 8, 2048, 1024], P('ens', None, None, 'slab')
Inputs may be any that keep to these rules, and one draw needn't show every extreme that they name: `cutoffs`: row 0 lies in 256 to 511 and row 1 in 128 to 255; in every member some level has row 0 equal to 511 and some level has row 1 equal to 255.
All inputs are finite; a program needn't handle non-finite values.
Results may differ from a plain program's by a relative error of at most 0.0003.
Values sent between devices are 32-bit elements; how exact they have to be, the bound alone decides.
No kernel may reach another device: no remote copies, remote signals or barrier semaphores. Data moves between devices by JAX's collectives and lax.ppermute only.
A program may use at most 128 MiB of HBM per device.

v0:
```python
import jax
import jax.numpy as jnp
import ml_dtypes
import numpy as np
from jax import lax
from jax.experimental import pallas as pl
from jax.experimental.pallas import tpu as pltpu
from jax.sharding import Mesh
from jax.sharding import PartitionSpec as P

NX = 2048
NY = 1024
KX = 512
KY = 256
COMP = 3
Z = 8
DEVICES = 64
ROWS = NX // DEVICES
SLAB = ("slab_0", "slab_1", "slab_2")

PIECE = (6, 8, 128)
QUARTER = NX // 4
READY = (0, 20, 42, 64)
F32 = jnp.float32
BF16 = jnp.bfloat16
VMEM = pltpu.MemorySpace.VMEM
SMEM = pltpu.MemorySpace.SMEM
HBM = pltpu.MemorySpace.HBM


def halves(x):
    high = x.astype(BF16)
    return high, (x - high.astype(F32)).astype(BF16)


def dot3(left, right):
    def one(a, b):
        return jnp.dot(a, b, preferred_element_type=F32)

    (lh, ll), (rh, rl) = left, right
    return one(lh, rh) + (one(ll, rh) + one(lh, rl))


def basis_y():
    parity = np.arange(2)[:, None, None]
    place = np.arange(NY // 2)[None, :, None]
    column = np.arange(KY)[None, None, :]
    phase = (place * (2 * (column % 128) + parity)) % NY
    angle = phase * (2.0 * np.pi / NY)
    table = np.where(column < 128, np.cos(angle), np.sin(angle))
    high = table.astype(ml_dtypes.bfloat16)
    low = (table - high.astype(np.float64)).astype(ml_dtypes.bfloat16)
    return np.stack([high, low], axis=1)


GROUPS = (0, 2, 1, 3)


def turns(left, right):
    phase = (left * right) % NX
    angle = phase * (2.0 * np.pi / NX)
    return np.stack([np.cos(angle), np.sin(angle)]).astype(np.float32)


def angle_parts():
    place = np.arange(QUARTER)[None, :]
    sixteen = np.arange(16)[:, None]
    coarse = turns(64 * np.arange(8)[:, None], place)
    fine = np.stack([turns(4 * sixteen + g, place) for g in GROUPS])
    wave = 4 * np.arange(128)[None, :]
    far = np.stack([turns(wave + g, 16 * np.arange(32)[:, None]) for g in GROUPS])
    near = np.stack([turns(wave + g, sixteen) for g in GROUPS])
    return coarse, fine, far, near


def products(a, b):
    return a[0] * b[0] - a[1] * b[1], a[1] * b[0] + a[0] * b[1]


def store(high_ref, low_ref, rows, columns, value):
    high_ref[rows, columns], low_ref[rows, columns] = halves(value)


def rows_of_waves(n_ref, ca_ref, fi_ref, fh_ref, fl_ref, t_ref):
    at = n_ref[1]
    plane = lax.broadcasted_iota(jnp.int32, (16, QUARTER), 1) == at % QUARTER

    def picked(value):
        return jnp.sum(jnp.where(plane, value, 0.0), axis=1, keepdims=True)

    for g in range(4):
        fine = fi_ref[g, 0], fi_ref[g, 1]
        turn = at // QUARTER * GROUPS[g] % 4
        cosine = jnp.where(turn % 2 == 0, 1 - turn, 0).astype(F32)
        sine = jnp.where(turn % 2 == 1, 2 - turn, 0).astype(F32)
        for n in range(8):
            coarse = ca_ref[0, n : n + 1], ca_ref[1, n : n + 1]
            first = 256 * g + 16 * n
            pair = products(coarse, fine)
            for i in range(2):
                rows = slice(first + 128 * i, first + 128 * i + 16)
                store(fh_ref, fl_ref, rows, slice(None), pair[i])
            c, s = picked(pair[0]), picked(pair[1])
            t_ref[first : first + 16] = jnp.broadcast_to(cosine * c - sine * s, (16, 128))
            t_ref[first + 128 : first + 144] = jnp.broadcast_to(sine * c + cosine * s, (16, 128))


def rows_of_places(fa_ref, ne_ref, ih_ref, il_ref):
    for g in range(4):
        near = ne_ref[g, 0], ne_ref[g, 1]
        for b in range(32):
            far = fa_ref[g, 0, b : b + 1], fa_ref[g, 1, b : b + 1]
            for i, value in enumerate(products(far, near)):
                first = 256 * g + 128 * i
                store(ih_ref, il_ref, slice(16 * b, 16 * b + 16), slice(first, first + 128), value)


def weights(n_ref, w_ref):
    def relax(place):
        offset = jnp.abs(place - n_ref[2])
        distance = jnp.minimum(offset, NX - offset)
        return jnp.exp(-distance.astype(F32) / (NX / 4.0))

    for g in range(8):
        place = 32 * (8 * g + lax.broadcasted_iota(jnp.int32, (8, 4, 8, 128), 0))
        place += 8 * lax.broadcasted_iota(jnp.int32, place.shape, 1)
        place += lax.broadcasted_iota(jnp.int32, place.shape, 2)
        w_ref[8 * g : 8 * g + 8, 0:4] = relax(place)
        rest = place[:, 0:2]
        w_ref[8 * g : 8 * g + 8, 4:6] = relax(jnp.where(half_lanes(rest), rest, rest + 16))


def half_lanes(x):
    return lax.broadcasted_iota(jnp.int32, (1,) * (x.ndim - 1) + (128,), x.ndim - 1) < 64


def swapped(x):
    return pltpu.roll(x, 64, x.ndim - 1)


def analysis_kernel(v_hbm, cut_hbm, table_hbm, o_hbm, o_ref, v_ref, cut_ref, table_ref, sems):
    copies = [
        pltpu.make_async_copy(table_hbm, table_ref, sems.at[COMP]),
        pltpu.make_async_copy(cut_hbm, cut_ref, sems.at[COMP + 1]),
    ]
    for c in range(COMP):
        fields = pl.ds(Z * c, Z)
        copies.append(
            pltpu.make_async_copy(v_hbm.at[fields], v_ref.at[fields], sems.at[c])
        )
    for copy in copies:
        copy.start()
    for copy in copies[:2]:
        copy.wait()
    lane = lax.broadcasted_iota(jnp.int32, (1, KY), 1) % 128
    for c in range(COMP):
        copies[2 + c].wait()
        field = v_ref[Z * c : Z * (c + 1)].reshape(Z * ROWS, NY)
        left, right = field[:, : NY // 2], field[:, NY // 2 :]
        for parity in range(2):
            folded = left - right if parity else left + right
            spectra = dot3(halves(folded), (table_ref[parity, 0], table_ref[parity, 1]))
            wave = 2 * lane + parity
            weight = jnp.where(wave == 0, 1.0 / NY, 2.0 / NY)
            for z in range(Z):
                scale = jnp.where(wave <= cut_ref[0, 1, z], weight, 0.0)
                own = spectra[ROWS * z : ROWS * (z + 1)] * scale
                for part in range(2):
                    block = 4 * (Z * c + z) + 2 * parity + part
                    values = own[:, 128 * part : 128 * (part + 1)]
                    first = block // 3 * 2
                    if block % 3 != 1:
                        o_ref[first + block % 3 // 2, 0:4] = values.reshape(4, 8, 128)
                        continue
                    above, below = values[:16], values[16:]
                    low = half_lanes(above)
                    even = jnp.where(low, above, swapped(below))
                    odd = jnp.where(low, swapped(above), below)
                    o_ref[first, 4:6] = even.reshape(2, 8, 128)
                    o_ref[first + 1, 4:6] = odd.reshape(2, 8, 128)
        ready = slice(READY[c], READY[c + 1])
        copies.append(
            pltpu.make_async_copy(o_ref.at[ready], o_hbm.at[ready], sems.at[COMP + 2 + c])
        )
        copies[-1].start()
    for copy in copies[2 + COMP :]:
        copy.wait()


def forward_kernel(n_ref, r_ref, ca_ref, fi_ref, c_ref, p_ref, fh_ref, fl_ref, t_ref):
    rows_of_waves(n_ref, ca_ref, fi_ref, fh_ref, fl_ref, t_ref)
    quarters = []
    for u in range(4):
        owned = slice(16 * u, 16 * (u + 1))
        main = r_ref[owned, 0:4].reshape(QUARTER, 128)
        rest = r_ref[owned, 4:6]
        rest = jnp.concatenate([rest, swapped(rest)], axis=1).reshape(QUARTER, 128)
        quarters.append(jnp.concatenate([main, rest], axis=1))
    v0, v1, v2, v3 = quarters
    even, odd = v0 + v2, v1 + v3
    inputs = [halves(even + odd), halves(even - odd), halves(v0 - v2), halves(v1 - v3)]

    def ahead(rows, data):
        return dot3((fh_ref[rows], fl_ref[rows]), data)

    x0 = ahead(slice(0, 256), inputs[0])
    x2 = ahead(slice(256, 512), inputs[1])
    yc = ahead(slice(512, 1024), inputs[2])
    yd = ahead(slice(512, 1024), inputs[3])
    device = n_ref[0]
    pair = device // 2
    whole = (3 * pair + 2 * (device % 2)) // 4 % Z
    shared = (3 * pair + 1) // 4 % Z
    lane = lax.broadcasted_iota(jnp.int32, (1, 256), 1)
    cut = jnp.where(lane < 128, n_ref[3 + whole], n_ref[3 + shared])
    index = lax.broadcasted_iota(jnp.int32, (128, 1), 0)

    def kept(values, group):
        wave = 4 * index + group
        weight = jnp.where(wave == 0, 1.0 / NX, 2.0 / NX)
        return jnp.where(wave <= cut, values * weight, 0.0)

    def part(values, i):
        return values[128 * i : 128 * (i + 1)]

    re1 = kept(part(yc, 0) - part(yd, 1), 1)
    im1 = kept(part(yc, 1) + part(yd, 0), 1)
    re3 = kept(part(yc, 2) + part(yd, 3), 3)
    im3 = kept(part(yc, 3) - part(yd, 2), 3)

    coeffs = jnp.concatenate(
        [
            kept(part(x0, 0), 0),
            kept(part(x0, 1), 0),
            kept(part(x2, 0), 2),
            kept(part(x2, 1), 2),
            re1,
            im1,
            re3,
            im3,
        ],
        axis=0,
    )
    c_ref[0], c_ref[1] = halves(coeffs)
    column = t_ref[...]
    row = jnp.concatenate(
        [jnp.sum(column * coeffs[:, 128 * i : 128 * (i + 1)], axis=0, keepdims=True) for i in range(2)],
        axis=1,
    )
    p_ref[...] = jnp.broadcast_to(row, (8, 256))


def inverse_kernel(n_ref, c_ref, fa_ref, ne_ref, o_ref, w_ref, ih_ref, il_ref):
    rows_of_places(fa_ref, ne_ref, ih_ref, il_ref)
    weights(n_ref, w_ref)

    def back(columns, data):
        return dot3((ih_ref[:, columns], il_ref[:, columns]), data)

    def rows(i, first, last):
        return c_ref[i, 128 * first : 128 * last]

    p0 = back(slice(0, 256), (rows(0, 0, 2), rows(1, 0, 2)))
    p2 = back(slice(256, 512), (rows(0, 2, 4), rows(1, 2, 4)))
    co = back(slice(512, 1024), (rows(0, 4, 8), rows(1, 4, 8)))
    turned = [
        jnp.concatenate([rows(i, 5, 6), -rows(i, 4, 5), -rows(i, 7, 8), rows(i, 6, 7)], axis=0)
        for i in range(2)
    ]
    do = back(slice(512, 1024), turned)
    even, odd = p0 + p2, p0 - p2
    for u, value in enumerate((even + co, odd + do, even - co, odd - do)):
        owned = slice(16 * u, 16 * (u + 1))
        o_ref[owned, 0:4] = value[:, :128].reshape(16, 4, 8, 128)
        rest = value[:, 128:].reshape(16, 4, 8, 128)
        above, below = rest[:, 0:2], rest[:, 2:4]
        o_ref[owned, 4:6] = jnp.where(half_lanes(above), above, swapped(below))


def blend_kernel(s_ref, w_ref, p_ref, o_ref):
    whole = p_ref[0:1, :128]
    shared = p_ref[0:1, 128:]
    shared = jnp.where(half_lanes(shared), shared, swapped(shared))
    for tiles, inflow in ((slice(0, 4), whole), (slice(4, 6), shared)):
        smooth = s_ref[:, tiles]
        o_ref[:, tiles] = smooth + w_ref[:, tiles] * (inflow[None, None] - smooth)


def synthesis_kernel(q_ref, table_ref, o_hbm, o_ref, sems):
    copies = []
    for c in range(COMP):
        sums = []
        for parity in range(2):
            rows = []
            for z in range(Z):
                blocks = []
                for part in range(2):
                    block = 4 * (Z * c + z) + 2 * parity + part
                    first = block // 3 * 2
                    if block % 3 != 1:
                        blocks.append(q_ref[first + block % 3 // 2, 0:4].reshape(ROWS, 128))
                        continue
                    even = q_ref[first, 4:6].reshape(16, 128)
                    odd = q_ref[first + 1, 4:6].reshape(16, 128)
                    low = half_lanes(even)
                    above = jnp.where(low, even, swapped(odd))
                    below = jnp.where(low, swapped(even), odd)
                    blocks.append(jnp.concatenate([above, below], axis=0))
                rows.append(jnp.concatenate(blocks, axis=1))
            data = halves(jnp.concatenate(rows, axis=0))
            sums.append(dot3(data, (table_ref[parity, 0], table_ref[parity, 1])))
        fields = slice(Z * c, Z * (c + 1))
        o_ref[fields, :, : NY // 2] = (sums[0] + sums[1]).reshape(Z, ROWS, NY // 2)
        o_ref[fields, :, NY // 2 :] = (sums[0] - sums[1]).reshape(Z, ROWS, NY // 2)
        fields = pl.ds(Z * c, Z)
        copies.append(
            pltpu.make_async_copy(o_ref.at[fields], o_hbm.at[fields], sems.at[c])
        )
        copies[-1].start()
    for copy in copies:
        copy.wait()


def whole(space):
    return pl.BlockSpec(memory_space=space)


def params(mib):
    return pltpu.CompilerParams(vmem_limit_bytes=mib * 1024 * 1024)


def shape(*dims, kind=F32):
    return jax.ShapeDtypeStruct(dims, kind)


PIECES = shape(DEVICES, *PIECE)
FIELDS = (COMP * Z, ROWS, NY)


def on_device(velocity, cutoffs, plane_index, boundary_index):
    table_y = basis_y()
    spectra = pl.pallas_call(
        analysis_kernel,
        in_specs=[whole(HBM)] * 3,
        out_specs=whole(HBM),
        out_shape=PIECES,
        scratch_shapes=[
            pltpu.VMEM(PIECES.shape, F32),
            pltpu.VMEM(FIELDS, F32),
            pltpu.SMEM((1, 2, Z), jnp.int32),
            pltpu.VMEM((2, 2, NY // 2, KY), BF16),
            pltpu.SemaphoreType.DMA((2 * COMP + 2,)),
        ],
        compiler_params=params(63),
        name="analysis",
    )(velocity.reshape(FIELDS), cutoffs, jnp.asarray(table_y))
    columns = lax.all_to_all(spectra, SLAB, 0, 0, tiled=True)
    device = lax.axis_index(SLAB).astype(jnp.int32).reshape(1)
    numbers = jnp.concatenate([device, plane_index, boundary_index, cutoffs[0, 0]])
    coarse, fine, far, near = (jnp.asarray(part) for part in angle_parts())
    coeffs, plane = pl.pallas_call(
        forward_kernel,
        in_specs=[whole(SMEM)] + [whole(VMEM)] * 3,
        out_specs=[whole(VMEM)] * 2,
        out_shape=[shape(2, 2 * KX, 256, kind=BF16), shape(8, 256)],
        scratch_shapes=[pltpu.VMEM((2 * KX, QUARTER), BF16)] * 2 + [pltpu.VMEM((2 * KX, 128), F32)],
        compiler_params=params(24),
        name="forward",
    )(numbers, columns, coarse, fine)
    members = lax.axis_size("ens")
    route = [((i - 1) % members, i) for i in range(members)]
    inflow = lax.ppermute(plane, "ens", route)
    smooth, weight = pl.pallas_call(
        inverse_kernel,
        in_specs=[whole(SMEM)] + [whole(VMEM)] * 3,
        out_specs=[whole(VMEM)] * 2,
        out_shape=[PIECES] * 2,
        scratch_shapes=[pltpu.VMEM((QUARTER, 2 * KX), BF16)] * 2,
        compiler_params=params(24),
        cost_estimate=pl.CostEstimate(flops=1 << 30, bytes_accessed=1 << 22, transcendentals=0),
        name="inverse",
    )(numbers, coeffs, far, near)
    blended = pl.pallas_call(
        blend_kernel,
        in_specs=[whole(VMEM)] * 3,
        out_specs=whole(VMEM),
        out_shape=PIECES,
        compiler_params=params(8),
        name="blend",
    )(smooth, weight, inflow)
    returned = lax.all_to_all(blended, SLAB, 0, 0, tiled=True)
    result = pl.pallas_call(
        synthesis_kernel,
        in_specs=[whole(VMEM), whole(VMEM)],
        out_specs=whole(HBM),
        out_shape=shape(*FIELDS),
        scratch_shapes=[pltpu.VMEM(FIELDS, F32), pltpu.SemaphoreType.DMA((COMP,))],
        compiler_params=params(24),
        name="synthesis",
    )(returned, jnp.asarray(table_y.transpose(0, 1, 3, 2)))
    return result.reshape(1, COMP, Z, ROWS, NY)


def solution(mesh):
    split = Mesh(
        mesh.devices.reshape(mesh.shape["ens"], 4, 8, 2), ("ens", "slab_0", "slab_1", "slab_2")
    )
    in_specs = (P("ens", None, None, SLAB, None), P("ens", None, None), P("ens"), P("ens"))
    out_specs = P("ens", None, None, SLAB, None)
    return jax.shard_map(
        on_device, mesh=split, in_specs=in_specs, out_specs=out_specs, check_vma=False
    )
```

profile of v0, /device:TPU:1, one launch (start us, length us, event | category | flops | bytes accessed | tf_op | source)
XLA Modules:
  0.0 113.5 jit_solution(10622823905665844483)
XLA Ops:
  0.0 4.4 %analysis.1 = f32[64,6,8,128]{3,2,1,0:T(8,128)} custom-call(f32[24,32,1024]{2,1,0:T(8,128)} %bitcast.5, s32[1,2,8]{2,1,0:T(2,128)} %cut_hbm.1, bf16[2,2,512,256]{3,2,1,0:T(8,128)(2,1)} %constant.30.clone.table_hbm), custom_call_target="tpu_custom_call" | custom-call | tf_op jit(solution)/shard_map/analysis/pallas_call | solution.py:342
  4.4 0.0 copy-start.5
  4.4 0.0 copy-start.1
  4.4 0.0 copy-start.2
  4.4 13.3 %all-to-all-start = ((f32[64,6,8,128]{3,2,1,0:T(8,128)}), f32[64,6,8,128]{3,2,1,0:T(8,128)S(1)}, u32[]{:S(2)}, u32[]{:S(2)}) async-start(f32[64,6,8,128]{3,2,1,0:T(8,128)} %analysis.1), calls=%async_computation | async-start | bytes 3145728 | tf_op jit(solution)/shard_map/all_to_all | solution.py:357
  17.7 0.0 copy-start.3
  17.7 0.0 copy-start.4
  19.1 0.0 copy-done.5
  19.1 0.1 pad_add_fusion.n_ref
  19.2 38.3 %all-to-all-done.r_ref = f32[64,6,8,128]{3,2,1,0:T(8,128)S(1)} async-done(((f32[64,6,8,128]{3,2,1,0:T(8,128)}), f32[64,6,8,128]{3,2,1,0:T(8,128)S(1)}, u32[]{:S(2)}, u32[]{:S(2)}) %all-to-all-start) | async-done | bytes 1572896 | tf_op jit(solution)/shard_map/all_to_all | solution.py:357
  57.5 0.0 copy-done.1
  57.5 0.0 copy-done.2
  57.5 2.4 %forward.1 = (bf16[2,1024,256]{2,1,0:T(8,128)(2,1)S(1)}, f32[8,256]{1,0:T(8,128)S(1)}) custom-call(s32[11]{0:T(128)S(1)} %pad_add_fusion.n_ref, f32[64,6,8,128]{3,2,1,0:T(8,128)S(1)} %all-to-all-done.r_ref, f32[2,8,512]{2,1,0:T(8,128)S(1)} %copy-done.2, f32[4,2,16,512]{3,2,1,0:T(8,128)S(1)} %copy-done.1), custom_call_target="tpu_custom_call" | custom-call | tf_op jit(solution)/shard_map/forward/pallas_call | solution.py:361
  59.9 1.3 %collective-permute-start = (f32[8,256]{1,0:T(8,128)S(1)}, f32[8,256]{1,0:T(8,128)S(1)}, u32[]{:S(2)}, u32[]{:S(2)}) collective-permute-start(f32[8,256]{1,0:T(8,128)S(1)} %get-tuple-element.12), channel_id=1, source_target_pairs={{192,0},{0,64},{64,128},{128,192},{193,1},{1,65},{65,129},{129,193... | collective-permute-start | bytes 24584 | tf_op jit(solution)/shard_map/ppermute | solution.py:372
  61.2 0.0 copy-done.3
  61.2 0.0 copy-done.4
  61.2 2.9 %inverse.1 = (f32[64,6,8,128]{3,2,1,0:T(8,128)S(1)}, f32[64,6,8,128]{3,2,1,0:T(8,128)S(1)}) custom-call(s32[11]{0:T(128)S(1)} %pad_add_fusion.n_ref, bf16[2,1024,256]{2,1,0:T(8,128)(2,1)S(1)} %get-tuple-element.9.c_ref, f32[4,2,32,128]{3,2,1,0:T(8,128)S(1)} %copy-done.3, f32[4,2,16,128]{3,2,1,0:T(8,128)S(1)} %copy-done.4), custom_call_target="tpu_custom_call" | custom-call | flops 1073741824 | bytes 4194304 | tf_op jit(solution)/shard_map/inverse/pallas_call | solution.py:373
  64.0 0.0 collective-permute-done.p_ref
  64.1 0.4 blend.1
  64.5 0.0 copy-start
  64.5 46.5 %all_to_all.10.q_ref = f32[64,6,8,128]{3,2,1,0:T(8,128)S(1)} all-to-all(f32[64,6,8,128]{3,2,1,0:T(8,128)S(1)} %blend.1), channel_id=1, replica_groups=mesh['ens'=4,'slab_0'=4,'slab_1'=8,'slab_2'=2] {'slab_0','slab_1','slab_2'}, dimensions={0} | all-to-all | bytes 3145728 | tf_op jit(solution)/shard_map/all_to_all | solution.py:391
  111.0 0.0 copy-done
  111.0 2.4 %synthesis.1 = f32[24,32,1024]{2,1,0:T(8,128)} custom-call(f32[64,6,8,128]{3,2,1,0:T(8,128)S(1)} %all_to_all.10.q_ref, bf16[2,2,256,512]{3,2,1,0:T(8,128)(2,1)S(1)} %copy-done), custom_call_target="tpu_custom_call" | custom-call | tf_op jit(solution)/shard_map/synthesis/pallas_call | solution.py:392
  (1 shorter events, 0.0 us)
Async XLA Ops:
  4.4 14.7 %copy-start.5 = (s32[1,2,8]{2,1,0:T(2,128)S(1)}, s32[1,2,8]{2,1,0:T(2,128)}, u32[]{:S(2)}) copy-start(s32[1,2,8]{2,1,0:T(2,128)} %cut_hbm.1) | copy-start | bytes 196
  4.4 53.1 %copy-start.1 = (f32[4,2,16,512]{3,2,1,0:T(8,128)S(1)}, f32[4,2,16,512]{3,2,1,0:T(8,128)}, u32[]{:S(2)}) copy-start(f32[4,2,16,512]{3,2,1,0:T(8,128)} %constant.32.clone.fi_ref) | copy-start | bytes 786436
  4.4 53.1 %copy-start.2 = (f32[2,8,512]{2,1,0:T(8,128)S(1)}, f32[2,8,512]{2,1,0:T(8,128)}, u32[]{:S(2)}) copy-start(f32[2,8,512]{2,1,0:T(8,128)} %constant.31.clone.ca_ref) | copy-start | bytes 98308
  4.4 53.1 %all-to-all-start = ((f32[64,6,8,128]{3,2,1,0:T(8,128)}), f32[64,6,8,128]{3,2,1,0:T(8,128)S(1)}, u32[]{:S(2)}, u32[]{:S(2)}) async-start(f32[64,6,8,128]{3,2,1,0:T(8,128)} %analysis.1), calls=%async_computation | async-start | bytes 3145728 | tf_op jit(solution)/shard_map/all_to_all | solution.py:357
  17.7 43.5 %copy-start.3 = (f32[4,2,32,128]{3,2,1,0:T(8,128)S(1)}, f32[4,2,32,128]{3,2,1,0:T(8,128)}, u32[]{:S(2)}) copy-start(f32[4,2,32,128]{3,2,1,0:T(8,128)} %constant.33.clone.fa_ref) | copy-start | bytes 393220
  17.7 43.5 %copy-start.4 = (f32[4,2,16,128]{3,2,1,0:T(8,128)S(1)}, f32[4,2,16,128]{3,2,1,0:T(8,128)}, u32[]{:S(2)}) copy-start(f32[4,2,16,128]{3,2,1,0:T(8,128)} %constant.34.clone.ne_ref) | copy-start | bytes 196612
  59.9 4.2 %collective-permute-start = (f32[8,256]{1,0:T(8,128)S(1)}, f32[8,256]{1,0:T(8,128)S(1)}, u32[]{:S(2)}, u32[]{:S(2)}) collective-permute-start(f32[8,256]{1,0:T(8,128)S(1)} %get-tuple-element.12), channel_id=1, source_target_pairs={{192,0},{0,64},{64,128},{128,192},{193,1},{1,65},{65,129},{129,193... | collective-permute-start | bytes 24584 | tf_op jit(solution)/shard_map/ppermute | solution.py:372
  64.5 46.6 %copy-start = (bf16[2,2,256,512]{3,2,1,0:T(8,128)(2,1)S(1)}, bf16[2,2,256,512]{3,2,1,0:T(8,128)(2,1)}, u32[]{:S(2)}) copy-start(bf16[2,2,256,512]{3,2,1,0:T(8,128)(2,1)} %constant.35.clone.table_ref) | copy-start | bytes 3145732
where the time goes:
time: 114 us; the launch traced here: 113 us
  blocking collectives  46.5 us (41%)
  waiting for transfers between devices  38.3 us (34%)
  starting transfers between devices  14.6 us (13%)
  Pallas kernels  12.5 us (11%)
  between operations  1.45 us (1%)
    all_to_all x1, blocking collectives, on_device(): returned = lax.all_to_all(blended, SLAB, 0, 0, tiled=True)  46.5 us
    all_to_all x1, waiting for transfers between devices, on_device(): columns = lax.all_to_all(spectra, SLAB, 0, 0, tiled=True)  38.3 us
    all_to_all x1, starting transfers between devices, on_device(): columns = lax.all_to_all(spectra, SLAB, 0, 0, tiled=True)  13.3 us
    pallas_call x1, Pallas kernels, on_device(): pl.pallas_call(analysis_kernel, in_specs=[whole(HBM)] * 3, out_specs=whol...  4.36 us
    pallas_call x1, Pallas kernels, on_device(): pl.pallas_call(inverse_kernel, in_specs=[whole(SMEM)] + [whole(VMEM)] * 3...  2.87 us
    pallas_call x1, Pallas kernels, on_device(): pl.pallas_call(synthesis_kernel, in_specs=[whole(VMEM), whole(VMEM)], out...  2.43 us
    pallas_call x1, Pallas kernels, on_device(): pl.pallas_call(forward_kernel, in_specs=[whole(SMEM)] + [whole(VMEM)] * 3...  2.4 us
  transfers between devices with their start and end apart: 2, of which 1 were waited for; matrix products, arithmetic and copies ran while one was open for 0% of the time, Pallas kernels for 3%

commit v1 on v0

--- a/solution.py
+++ b/solution.py
@@ -20,7 +20,7 @@
 
 PIECE = (6, 8, 128)
 QUARTER = NX // 4
-READY = (0, 20, 42, 64)
+CHUNKS = ((0, 8), (8, 16), (16, 20), (20, 24))
 F32 = jnp.float32
 BF16 = jnp.bfloat16
 VMEM = pltpu.MemorySpace.VMEM
@@ -43,22 +43,28 @@
 
 def basis_y():
     parity = np.arange(2)[:, None, None]
-    place = np.arange(NY // 2)[None, :, None]
-    column = np.arange(KY)[None, None, :]
-    phase = (place * (2 * (column % 128) + parity)) % NY
+    row = np.arange(KY)[None, :, None]
+    place = np.arange(NY // 2)[None, None, :]
+    phase = (place * (2 * (row % 128) + parity)) % NY
     angle = phase * (2.0 * np.pi / NY)
-    table = np.where(column < 128, np.cos(angle), np.sin(angle))
+    table = np.where(row < 128, np.cos(angle), np.sin(angle))
     high = table.astype(ml_dtypes.bfloat16)
     low = (table - high.astype(np.float64)).astype(ml_dtypes.bfloat16)
     return np.stack([high, low], axis=1)
 
 
+def parts_y():
+    wave = 2 * np.arange(128)[None, :]
+    place = np.concatenate([16 * np.arange(32), np.arange(16)])[:, None]
+    return np.stack([turns(wave + parity, place, NY) for parity in range(2)])
+
+
 GROUPS = (0, 2, 1, 3)
 
 
-def turns(left, right):
-    phase = (left * right) % NX
-    angle = phase * (2.0 * np.pi / NX)
+def turns(left, right, length=NX):
+    phase = (left * right) % length
+    angle = phase * (2.0 * np.pi / length)
     return np.stack([np.cos(angle), np.sin(angle)]).astype(np.float32)
 
 
@@ -81,28 +87,30 @@
     high_ref[rows, columns], low_ref[rows, columns] = halves(value)
 
 
-def rows_of_waves(n_ref, ca_ref, fi_ref, fh_ref, fl_ref, t_ref):
-    at = n_ref[1]
-    plane = lax.broadcasted_iota(jnp.int32, (16, QUARTER), 1) == at % QUARTER
+def rows_of_waves(plane_ref, ca_ref, fi_ref, fh_ref, fl_ref, t_ref):
+    at = plane_ref[0]
 
     def picked(value):
-        return jnp.sum(jnp.where(plane, value, 0.0), axis=1, keepdims=True)
-
+        here = lax.broadcasted_iota(jnp.int32, value.shape, 1) == at % QUARTER
+        return jnp.sum(jnp.where(here, value, 0.0), axis=1, keepdims=True)
+
+    coarse_at = picked(ca_ref[0]), picked(ca_ref[1])
     for g in range(4):
         fine = fi_ref[g, 0], fi_ref[g, 1]
         turn = at // QUARTER * GROUPS[g] % 4
         cosine = jnp.where(turn % 2 == 0, 1 - turn, 0).astype(F32)
         sine = jnp.where(turn % 2 == 1, 2 - turn, 0).astype(F32)
+        c, s = picked(fine[0]), picked(fine[1])
+        fine_at = cosine * c - sine * s, sine * c + cosine * s
         for n in range(8):
             coarse = ca_ref[0, n : n + 1], ca_ref[1, n : n + 1]
-            first = 256 * g + 16 * n
-            pair = products(coarse, fine)
+            there = coarse_at[0][n : n + 1], coarse_at[1][n : n + 1]
+            values, at_plane = products(coarse, fine), products(there, fine_at)
             for i in range(2):
-                rows = slice(first + 128 * i, first + 128 * i + 16)
-                store(fh_ref, fl_ref, rows, slice(None), pair[i])
-            c, s = picked(pair[0]), picked(pair[1])
-            t_ref[first : first + 16] = jnp.broadcast_to(cosine * c - sine * s, (16, 128))
-            t_ref[first + 128 : first + 144] = jnp.broadcast_to(sine * c + cosine * s, (16, 128))
+                first = 256 * g + 128 * i + 16 * n
+                rows = slice(first, first + 16)
+                store(fh_ref, fl_ref, rows, slice(None), values[i])
+                t_ref[rows] = jnp.broadcast_to(at_plane[i], (16, 128))
 
 
 def rows_of_places(fa_ref, ne_ref, ih_ref, il_ref):
@@ -115,9 +123,9 @@
                 store(ih_ref, il_ref, slice(16 * b, 16 * b + 16), slice(first, first + 128), value)
 
 
-def weights(n_ref, w_ref):
+def weights(bound_ref, w_ref):
     def relax(place):
-        offset = jnp.abs(place - n_ref[2])
+        offset = jnp.abs(place - bound_ref[0])
         distance = jnp.minimum(offset, NX - offset)
         return jnp.exp(-distance.astype(F32) / (NX / 4.0))
 
@@ -138,35 +146,47 @@
     return pltpu.roll(x, 64, x.ndim - 1)
 
 
-def analysis_kernel(v_hbm, cut_hbm, table_hbm, o_hbm, o_ref, v_ref, cut_ref, table_ref, sems):
+def analysis_kernel(
+    v_hbm, cut_hbm, part_hbm, o_hbm, o_ref, v_ref, cut_ref, part_ref, table_ref, sems
+):
     copies = [
-        pltpu.make_async_copy(table_hbm, table_ref, sems.at[COMP]),
-        pltpu.make_async_copy(cut_hbm, cut_ref, sems.at[COMP + 1]),
+        pltpu.make_async_copy(part_hbm, part_ref, sems.at[0]),
+        pltpu.make_async_copy(cut_hbm, cut_ref, sems.at[1]),
     ]
-    for c in range(COMP):
-        fields = pl.ds(Z * c, Z)
+    for i, (first, last) in enumerate(CHUNKS):
+        fields = pl.ds(first, last - first)
         copies.append(
-            pltpu.make_async_copy(v_hbm.at[fields], v_ref.at[fields], sems.at[c])
+            pltpu.make_async_copy(v_hbm.at[fields], v_ref.at[fields], sems.at[2 + i])
         )
     for copy in copies:
         copy.start()
     for copy in copies[:2]:
         copy.wait()
+    for parity in range(2):
+        near = part_ref[parity, 0, 32:48], part_ref[parity, 1, 32:48]
+        for b in range(32):
+            far = part_ref[parity, 0, b : b + 1], part_ref[parity, 1, b : b + 1]
+            for i, value in enumerate(products(far, near)):
+                rows, columns = slice(16 * b, 16 * b + 16), slice(128 * i, 128 * i + 128)
+                high, low = halves(value)
+                table_ref[parity, 0, rows, columns] = high
+                table_ref[parity, 1, rows, columns] = low
     lane = lax.broadcasted_iota(jnp.int32, (1, KY), 1) % 128
-    for c in range(COMP):
-        copies[2 + c].wait()
-        field = v_ref[Z * c : Z * (c + 1)].reshape(Z * ROWS, NY)
+    sent = 0
+    for i, (begin, end) in enumerate(CHUNKS):
+        copies[2 + i].wait()
+        field = v_ref[begin:end].reshape((end - begin) * ROWS, NY)
         left, right = field[:, : NY // 2], field[:, NY // 2 :]
         for parity in range(2):
             folded = left - right if parity else left + right
             spectra = dot3(halves(folded), (table_ref[parity, 0], table_ref[parity, 1]))
             wave = 2 * lane + parity
             weight = jnp.where(wave == 0, 1.0 / NY, 2.0 / NY)
-            for z in range(Z):
-                scale = jnp.where(wave <= cut_ref[0, 1, z], weight, 0.0)
-                own = spectra[ROWS * z : ROWS * (z + 1)] * scale
+            for f in range(begin, end):
+                scale = jnp.where(wave <= cut_ref[0, 1, f % Z], weight, 0.0)
+                own = spectra[ROWS * (f - begin) : ROWS * (f - begin + 1)] * scale
                 for part in range(2):
-                    block = 4 * (Z * c + z) + 2 * parity + part
+                    block = 4 * f + 2 * parity + part
                     values = own[:, 128 * part : 128 * (part + 1)]
                     first = block // 3 * 2
                     if block % 3 != 1:
@@ -178,17 +198,19 @@
                     odd = jnp.where(low, swapped(above), below)
                     o_ref[first, 4:6] = even.reshape(2, 8, 128)
                     o_ref[first + 1, 4:6] = odd.reshape(2, 8, 128)
-        ready = slice(READY[c], READY[c + 1])
-        copies.append(
-            pltpu.make_async_copy(o_ref.at[ready], o_hbm.at[ready], sems.at[COMP + 2 + c])
+        ready = pl.ds(sent, 4 * end // 3 * 2 - sent)
+        sent = 4 * end // 3 * 2
+        done = pltpu.make_async_copy(
+            o_ref.at[ready], o_hbm.at[ready], sems.at[2 + len(CHUNKS) + i]
         )
-        copies[-1].start()
-    for copy in copies[2 + COMP :]:
+        done.start()
+        copies.append(done)
+    for copy in copies[2 + len(CHUNKS) :]:
         copy.wait()
 
 
-def forward_kernel(n_ref, r_ref, ca_ref, fi_ref, c_ref, p_ref, fh_ref, fl_ref, t_ref):
-    rows_of_waves(n_ref, ca_ref, fi_ref, fh_ref, fl_ref, t_ref)
+def forward_kernel(cut_ref, plane_ref, r_ref, ca_ref, fi_ref, c_ref, p_ref, fh_ref, fl_ref, t_ref):
+    rows_of_waves(plane_ref, ca_ref, fi_ref, fh_ref, fl_ref, t_ref)
     quarters = []
     for u in range(4):
         owned = slice(16 * u, 16 * (u + 1))
@@ -207,12 +229,15 @@
     x2 = ahead(slice(256, 512), inputs[1])
     yc = ahead(slice(512, 1024), inputs[2])
     yd = ahead(slice(512, 1024), inputs[3])
-    device = n_ref[0]
-    pair = device // 2
-    whole = (3 * pair + 2 * (device % 2)) // 4 % Z
+    pair = 8 * lax.axis_index("slab_0") + lax.axis_index("slab_1")
+    whole = (3 * pair + 2 * lax.axis_index("slab_2")) // 4 % Z
     shared = (3 * pair + 1) // 4 % Z
     lane = lax.broadcasted_iota(jnp.int32, (1, 256), 1)
-    cut = jnp.where(lane < 128, n_ref[3 + whole], n_ref[3 + shared])
+    cuts = cut_ref[0, 0:1]
+    level = jnp.where(lane < 128, whole, shared)
+    cut = jnp.zeros((1, 256), jnp.int32)
+    for z in range(Z):
+        cut = jnp.where(level == z, cuts[:, z : z + 1], cut)
     index = lax.broadcasted_iota(jnp.int32, (128, 1), 0)
 
     def kept(values, group):
@@ -250,9 +275,9 @@
     p_ref[...] = jnp.broadcast_to(row, (8, 256))
 
 
-def inverse_kernel(n_ref, c_ref, fa_ref, ne_ref, o_ref, w_ref, ih_ref, il_ref):
+def inverse_kernel(bound_ref, c_ref, fa_ref, ne_ref, o_ref, w_ref, ih_ref, il_ref):
     rows_of_places(fa_ref, ne_ref, ih_ref, il_ref)
-    weights(n_ref, w_ref)
+    weights(bound_ref, w_ref)
 
     def back(columns, data):
         return dot3((ih_ref[:, columns], il_ref[:, columns]), data)
@@ -288,14 +313,14 @@
 
 def synthesis_kernel(q_ref, table_ref, o_hbm, o_ref, sems):
     copies = []
-    for c in range(COMP):
+    for i, (begin, end) in enumerate(CHUNKS):
         sums = []
         for parity in range(2):
             rows = []
-            for z in range(Z):
+            for f in range(begin, end):
                 blocks = []
                 for part in range(2):
-                    block = 4 * (Z * c + z) + 2 * parity + part
+                    block = 4 * f + 2 * parity + part
                     first = block // 3 * 2
                     if block % 3 != 1:
                         blocks.append(q_ref[first + block % 3 // 2, 0:4].reshape(ROWS, 128))
@@ -309,12 +334,12 @@
                 rows.append(jnp.concatenate(blocks, axis=1))
             data = halves(jnp.concatenate(rows, axis=0))
             sums.append(dot3(data, (table_ref[parity, 0], table_ref[parity, 1])))
-        fields = slice(Z * c, Z * (c + 1))
-        o_ref[fields, :, : NY // 2] = (sums[0] + sums[1]).reshape(Z, ROWS, NY // 2)
-        o_ref[fields, :, NY // 2 :] = (sums[0] - sums[1]).reshape(Z, ROWS, NY // 2)
-        fields = pl.ds(Z * c, Z)
+        dims = (end - begin, ROWS, NY // 2)
+        o_ref[begin:end, :, : NY // 2] = (sums[0] + sums[1]).reshape(dims)
+        o_ref[begin:end, :, NY // 2 :] = (sums[0] - sums[1]).reshape(dims)
+        fields = pl.ds(begin, end - begin)
         copies.append(
-            pltpu.make_async_copy(o_ref.at[fields], o_hbm.at[fields], sems.at[c])
+            pltpu.make_async_copy(o_ref.at[fields], o_hbm.at[fields], sems.at[i])
         )
         copies[-1].start()
     for copy in copies:
@@ -338,7 +363,6 @@
 
 
 def on_device(velocity, cutoffs, plane_index, boundary_index):
-    table_y = basis_y()
     spectra = pl.pallas_call(
         analysis_kernel,
         in_specs=[whole(HBM)] * 3,
@@ -348,25 +372,24 @@
             pltpu.VMEM(PIECES.shape, F32),
             pltpu.VMEM(FIELDS, F32),
             pltpu.SMEM((1, 2, Z), jnp.int32),
+            pltpu.VMEM((2, 2, 48, 128), F32),
             pltpu.VMEM((2, 2, NY // 2, KY), BF16),
-            pltpu.SemaphoreType.DMA((2 * COMP + 2,)),
+            pltpu.SemaphoreType.DMA((2 + 2 * len(CHUNKS),)),
         ],
         compiler_params=params(63),
         name="analysis",
-    )(velocity.reshape(FIELDS), cutoffs, jnp.asarray(table_y))
+    )(velocity.reshape(FIELDS), cutoffs, jnp.asarray(parts_y()))
     columns = lax.all_to_all(spectra, SLAB, 0, 0, tiled=True)
-    device = lax.axis_index(SLAB).astype(jnp.int32).reshape(1)
-    numbers = jnp.concatenate([device, plane_index, boundary_index, cutoffs[0, 0]])
     coarse, fine, far, near = (jnp.asarray(part) for part in angle_parts())
     coeffs, plane = pl.pallas_call(
         forward_kernel,
-        in_specs=[whole(SMEM)] + [whole(VMEM)] * 3,
+        in_specs=[whole(VMEM), whole(SMEM)] + [whole(VMEM)] * 3,
         out_specs=[whole(VMEM)] * 2,
         out_shape=[shape(2, 2 * KX, 256, kind=BF16), shape(8, 256)],
         scratch_shapes=[pltpu.VMEM((2 * KX, QUARTER), BF16)] * 2 + [pltpu.VMEM((2 * KX, 128), F32)],
         compiler_params=params(24),
         name="forward",
-    )(numbers, columns, coarse, fine)
+    )(cutoffs, plane_index, columns, coarse, fine)
     members = lax.axis_size("ens")
     route = [((i - 1) % members, i) for i in range(members)]
     inflow = lax.ppermute(plane, "ens", route)
@@ -379,7 +402,7 @@
         compiler_params=params(24),
         cost_estimate=pl.CostEstimate(flops=1 << 30, bytes_accessed=1 << 22, transcendentals=0),
         name="inverse",
-    )(numbers, coeffs, far, near)
+    )(boundary_index, coeffs, far, near)
     blended = pl.pallas_call(
         blend_kernel,
         in_specs=[whole(VMEM)] * 3,
@@ -394,10 +417,10 @@
         in_specs=[whole(VMEM), whole(VMEM)],
         out_specs=whole(HBM),
         out_shape=shape(*FIELDS),
-        scratch_shapes=[pltpu.VMEM(FIELDS, F32), pltpu.SemaphoreType.DMA((COMP,))],
+        scratch_shapes=[pltpu.VMEM(FIELDS, F32), pltpu.SemaphoreType.DMA((len(CHUNKS),))],
         compiler_params=params(24),
         name="synthesis",
-    )(returned, jnp.asarray(table_y.transpose(0, 1, 3, 2)))
+    )(returned, jnp.asarray(basis_y()))
     return result.reshape(1, COMP, Z, ROWS, NY)
 
 

time: 114 us -> 113 us (level)
  transfers between devices with their start and end apart: 2 -> 2, of which waited for: 1 -> 2; matrix products, arithmetic and copies ran while one was open for 0% -> 0% of each run, Pallas kernels for 3% -> 2%
where the time goes in v1:
time: 113 us
  blocking collectives  46.9 us (42%)
  waiting for transfers between devices  38.6 us (34%)
  starting transfers between devices  14.6 us (13%)
  Pallas kernels  11.4 us (10%)
  between operations  1.42 us (1%)
    all_to_all x1, blocking collectives, on_device(): returned = lax.all_to_all(blended, SLAB, 0, 0, tiled=True)  46.9 us
    all_to_all x1, waiting for transfers between devices, on_device(): columns = lax.all_to_all(spectra, SLAB, 0, 0, tiled=True)  38.4 us
    all_to_all x1, starting transfers between devices, on_device(): columns = lax.all_to_all(spectra, SLAB, 0, 0, tiled=True)  13.3 us
    pallas_call x1, Pallas kernels, on_device(): pl.pallas_call(analysis_kernel, in_specs=[whole(HBM)] * 3, out_specs=whol...  4.29 us
    pallas_call x1, Pallas kernels, on_device(): pl.pallas_call(synthesis_kernel, in_specs=[whole(VMEM), whole(VMEM)], out...  2.37 us
    pallas_call x1, Pallas kernels, on_device(): pl.pallas_call(inverse_kernel, in_specs=[whole(SMEM)] + [whole(VMEM)] * 3...  2.33 us
  transfers between devices with their start and end apart: 2, of which 2 were waited for; matrix products, arithmetic and copies ran while one was open for 0% of the time, Pallas kernels for 2%

profile of v1, /device:TPU:1, one launch (start us, length us, event | category | flops | bytes accessed | tf_op | source)
XLA Modules:
  0.0 112.9 jit_solution(1688683564541364343)
XLA Ops:
  0.0 4.3 %analysis.1 = f32[64,6,8,128]{3,2,1,0:T(8,128)} custom-call(f32[24,32,1024]{2,1,0:T(8,128)} %bitcast.2, s32[1,2,8]{2,1,0:T(2,128)} %cut_ref.1, f32[2,2,48,128]{3,2,1,0:T(8,128)} %constant.12.clone.part_hbm), custom_call_target="tpu_custom_call" | custom-call | tf_op jit(solution)/shard_map/analysis/pallas_call | solution.py:366
  4.3 0.0 copy-start.1
  4.3 0.0 copy-start.2
  4.3 0.0 copy-start.3
  4.3 13.3 %all-to-all-start = ((f32[64,6,8,128]{3,2,1,0:T(8,128)}), f32[64,6,8,128]{3,2,1,0:T(8,128)S(1)}, u32[]{:S(2)}, u32[]{:S(2)}) async-start(f32[64,6,8,128]{3,2,1,0:T(8,128)} %analysis.1), calls=%async_computation | async-start | bytes 3145728 | tf_op jit(solution)/shard_map/all_to_all | solution.py:382
  17.6 0.0 copy-start.4
  17.7 0.0 copy-start.5
  19.0 38.4 %all-to-all-done.r_ref = f32[64,6,8,128]{3,2,1,0:T(8,128)S(1)} async-done(((f32[64,6,8,128]{3,2,1,0:T(8,128)}), f32[64,6,8,128]{3,2,1,0:T(8,128)S(1)}, u32[]{:S(2)}, u32[]{:S(2)}) %all-to-all-start) | async-done | bytes 1572896 | tf_op jit(solution)/shard_map/all_to_all | solution.py:382
  57.4 0.0 copy-done.1
  57.4 0.0 copy-done.2
  57.4 0.0 copy-done.3
  57.4 1.9 %forward.1 = (bf16[2,1024,256]{2,1,0:T(8,128)(2,1)S(1)}, f32[8,256]{1,0:T(8,128)S(1)}) custom-call(s32[1,2,8]{2,1,0:T(2,128)S(1)} %copy-done.3, s32[1]{0:T(128)S(6)} %copy.11.plane_ref, f32[64,6,8,128]{3,2,1,0:T(8,128)S(1)} %all-to-all-done.r_ref, f32[2,8,512]{2,1,0:T(8,128)S(1)} %copy-done.2, f32[4,2,16,512]{3,2,1,0:T(8,128)S(1)} %copy-done.1), custom_call_target="tpu_custom_call" | custom-call | tf_op jit(solution)/shard_map/forward/pallas_call | solution.py:384
  59.4 1.3 %collective-permute-start = (f32[8,256]{1,0:T(8,128)S(1)}, f32[8,256]{1,0:T(8,128)S(1)}, u32[]{:S(2)}, u32[]{:S(2)}) collective-permute-start(f32[8,256]{1,0:T(8,128)S(1)} %get-tuple-element.12), channel_id=1, source_target_pairs={{192,0},{0,64},{64,128},{128,192},{193,1},{1,65},{65,129},{129,193... | collective-permute-start | bytes 24584 | tf_op jit(solution)/shard_map/ppermute | solution.py:395
  60.6 0.0 copy-done.4
  60.7 0.0 copy-done.5
  60.7 2.3 %inverse.1 = (f32[64,6,8,128]{3,2,1,0:T(8,128)S(1)}, f32[64,6,8,128]{3,2,1,0:T(8,128)S(1)}) custom-call(s32[1]{0:T(128)S(6)} %copy.12.bound_ref, bf16[2,1024,256]{2,1,0:T(8,128)(2,1)S(1)} %get-tuple-element.9.c_ref, f32[4,2,32,128]{3,2,1,0:T(8,128)S(1)} %copy-done.4, f32[4,2,16,128]{3,2,1,0:T(8,128)S(1)} %copy-done.5), custom_call_target="tpu_custom_call" | custom-call | flops 1073741824 | bytes 4194304 | tf_op jit(solution)/shard_map/inverse/pallas_call | solution.py:396
  63.0 0.2 collective-permute-done.p_ref
  63.1 0.4 blend.1
  63.6 0.0 copy-start
  63.6 46.9 %all_to_all.10.q_ref = f32[64,6,8,128]{3,2,1,0:T(8,128)S(1)} all-to-all(f32[64,6,8,128]{3,2,1,0:T(8,128)S(1)} %blend.1), channel_id=1, replica_groups=mesh['ens'=4,'slab_0'=4,'slab_1'=8,'slab_2'=2] {'slab_0','slab_1','slab_2'}, dimensions={0} | all-to-all | bytes 3145728 | tf_op jit(solution)/shard_map/all_to_all | solution.py:414
  110.5 0.0 copy-done
  110.5 2.4 %synthesis.1 = f32[24,32,1024]{2,1,0:T(8,128)} custom-call(f32[64,6,8,128]{3,2,1,0:T(8,128)S(1)} %all_to_all.10.q_ref, bf16[2,2,256,512]{3,2,1,0:T(8,128)(2,1)S(1)} %copy-done), custom_call_target="tpu_custom_call" | custom-call | tf_op jit(solution)/shard_map/synthesis/pallas_call | solution.py:415
Async XLA Ops:
  4.3 53.1 %copy-start.1 = (f32[4,2,16,512]{3,2,1,0:T(8,128)S(1)}, f32[4,2,16,512]{3,2,1,0:T(8,128)}, u32[]{:S(2)}) copy-start(f32[4,2,16,512]{3,2,1,0:T(8,128)} %constant.14.clone.fi_ref) | copy-start | bytes 786436
  4.3 53.1 %copy-start.2 = (f32[2,8,512]{2,1,0:T(8,128)S(1)}, f32[2,8,512]{2,1,0:T(8,128)}, u32[]{:S(2)}) copy-start(f32[2,8,512]{2,1,0:T(8,128)} %constant.13.clone.ca_ref) | copy-start | bytes 98308
  4.3 53.1 %copy-start.3 = (s32[1,2,8]{2,1,0:T(2,128)S(1)}, s32[1,2,8]{2,1,0:T(2,128)}, u32[]{:S(2)}) copy-start(s32[1,2,8]{2,1,0:T(2,128)} %cut_ref.1) | copy-start | bytes 196
  4.3 53.1 %all-to-all-start = ((f32[64,6,8,128]{3,2,1,0:T(8,128)}), f32[64,6,8,128]{3,2,1,0:T(8,128)S(1)}, u32[]{:S(2)}, u32[]{:S(2)}) async-start(f32[64,6,8,128]{3,2,1,0:T(8,128)} %analysis.1), calls=%async_computation | async-start | bytes 3145728 | tf_op jit(solution)/shard_map/all_to_all | solution.py:382
  17.6 43.0 %copy-start.4 = (f32[4,2,32,128]{3,2,1,0:T(8,128)S(1)}, f32[4,2,32,128]{3,2,1,0:T(8,128)}, u32[]{:S(2)}) copy-start(f32[4,2,32,128]{3,2,1,0:T(8,128)} %constant.15.clone.fa_ref) | copy-start | bytes 393220
  17.7 43.0 %copy-start.5 = (f32[4,2,16,128]{3,2,1,0:T(8,128)S(1)}, f32[4,2,16,128]{3,2,1,0:T(8,128)}, u32[]{:S(2)}) copy-start(f32[4,2,16,128]{3,2,1,0:T(8,128)} %constant.16.clone.ne_ref) | copy-start | bytes 196612
  59.4 3.8 %collective-permute-start = (f32[8,256]{1,0:T(8,128)S(1)}, f32[8,256]{1,0:T(8,128)S(1)}, u32[]{:S(2)}, u32[]{:S(2)}) collective-permute-start(f32[8,256]{1,0:T(8,128)S(1)} %get-tuple-element.12), channel_id=1, source_target_pairs={{192,0},{0,64},{64,128},{128,192},{193,1},{1,65},{65,129},{129,193... | collective-permute-start | bytes 24584 | tf_op jit(solution)/shard_map/ppermute | solution.py:395
  63.6 47.0 %copy-start = (bf16[2,2,256,512]{3,2,1,0:T(8,128)(2,1)S(1)}, bf16[2,2,256,512]{3,2,1,0:T(8,128)(2,1)}, u32[]{:S(2)}) copy-start(bf16[2,2,256,512]{3,2,1,0:T(8,128)(2,1)} %constant.17.clone.table_ref) | copy-start | bytes 3145732

commit v2 on v1

--- a/solution.py
+++ b/solution.py
@@ -20,7 +20,8 @@
 
 PIECE = (6, 8, 128)
 QUARTER = NX // 4
-CHUNKS = ((0, 8), (8, 16), (16, 20), (20, 24))
+CHUNKS = ((0, 8), (8, 16), (16, 24))
+CHUNKS_OUT = ((0, 4), (4, 8), (8, 12), (12, 16), (16, 20), (20, 24))
 F32 = jnp.float32
 BF16 = jnp.bfloat16
 VMEM = pltpu.MemorySpace.VMEM
@@ -266,7 +267,7 @@
         ],
         axis=0,
     )
-    c_ref[0], c_ref[1] = halves(coeffs)
+    c_ref[...] = coeffs
     column = t_ref[...]
     row = jnp.concatenate(
         [jnp.sum(column * coeffs[:, 128 * i : 128 * (i + 1)], axis=0, keepdims=True) for i in range(2)],
@@ -282,8 +283,10 @@
     def back(columns, data):
         return dot3((ih_ref[:, columns], il_ref[:, columns]), data)
 
+    split = halves(c_ref[...])
+
     def rows(i, first, last):
-        return c_ref[i, 128 * first : 128 * last]
+        return split[i][128 * first : 128 * last]
 
     p0 = back(slice(0, 256), (rows(0, 0, 2), rows(1, 0, 2)))
     p2 = back(slice(256, 512), (rows(0, 2, 4), rows(1, 2, 4)))
@@ -313,7 +316,7 @@
 
 def synthesis_kernel(q_ref, table_ref, o_hbm, o_ref, sems):
     copies = []
-    for i, (begin, end) in enumerate(CHUNKS):
+    for i, (begin, end) in enumerate(CHUNKS_OUT):
         sums = []
         for parity in range(2):
             rows = []
@@ -385,7 +388,7 @@
         forward_kernel,
         in_specs=[whole(VMEM), whole(SMEM)] + [whole(VMEM)] * 3,
         out_specs=[whole(VMEM)] * 2,
-        out_shape=[shape(2, 2 * KX, 256, kind=BF16), shape(8, 256)],
+        out_shape=[shape(2 * KX, 256), shape(8, 256)],
         scratch_shapes=[pltpu.VMEM((2 * KX, QUARTER), BF16)] * 2 + [pltpu.VMEM((2 * KX, 128), F32)],
         compiler_params=params(24),
         name="forward",
@@ -417,7 +420,7 @@
         in_specs=[whole(VMEM), whole(VMEM)],
         out_specs=whole(HBM),
         out_shape=shape(*FIELDS),
-        scratch_shapes=[pltpu.VMEM(FIELDS, F32), pltpu.SemaphoreType.DMA((len(CHUNKS),))],
+        scratch_shapes=[pltpu.VMEM(FIELDS, F32), pltpu.SemaphoreType.DMA((len(CHUNKS_OUT),))],
         compiler_params=params(24),
         name="synthesis",
     )(returned, jnp.asarray(basis_y()))

time: 113 us -> 113 us (level)
  no operation moved by 1% of the time
where the time goes in v2:
time: 113 us; the launch traced here: 112 us
  blocking collectives  46.9 us (42%)
  waiting for transfers between devices  38.5 us (34%)
  starting transfers between devices  14.6 us (13%)
  Pallas kernels  11 us (10%)
  between operations  1.41 us (1%)
    all_to_all x1, blocking collectives, on_device(): returned = lax.all_to_all(blended, SLAB, 0, 0, tiled=True)  46.9 us
    all_to_all x1, waiting for transfers between devices, on_device(): columns = lax.all_to_all(spectra, SLAB, 0, 0, tiled=True)  38.4 us
    all_to_all x1, starting transfers between devices, on_device(): columns = lax.all_to_all(spectra, SLAB, 0, 0, tiled=True)  13.3 us
    pallas_call x1, Pallas kernels, on_device(): pl.pallas_call(analysis_kernel, in_specs=[whole(HBM)] * 3, out_specs=whol...  4.1 us
    pallas_call x1, Pallas kernels, on_device(): pl.pallas_call(inverse_kernel, in_specs=[whole(SMEM)] + [whole(VMEM)] * 3...  2.37 us
    pallas_call x1, Pallas kernels, on_device(): pl.pallas_call(synthesis_kernel, in_specs=[whole(VMEM), whole(VMEM)], out...  2.29 us
  transfers between devices with their start and end apart: 2, of which 2 were waited for; matrix products, arithmetic and copies ran while one was open for 0% of the time, Pallas kernels for 2%

profile of v2, /device:TPU:1, one launch (start us, length us, event | category | flops | bytes accessed | tf_op | source)
XLA Modules:
  0.0 112.5 jit_solution(17544842641952978193)
XLA Ops:
  0.0 4.1 %analysis.1 = f32[64,6,8,128]{3,2,1,0:T(8,128)} custom-call(f32[24,32,1024]{2,1,0:T(8,128)} %bitcast.2, s32[1,2,8]{2,1,0:T(2,128)} %cut_ref.1, f32[2,2,48,128]{3,2,1,0:T(8,128)} %constant.12.clone.part_hbm), custom_call_target="tpu_custom_call" | custom-call | tf_op jit(solution)/shard_map/analysis/pallas_call | solution.py:369
  4.1 0.0 copy-start.1
  4.1 0.0 copy-start.2
  4.1 0.0 copy-start.3
  4.1 13.3 %all-to-all-start = ((f32[64,6,8,128]{3,2,1,0:T(8,128)}), f32[64,6,8,128]{3,2,1,0:T(8,128)S(1)}, u32[]{:S(2)}, u32[]{:S(2)}) async-start(f32[64,6,8,128]{3,2,1,0:T(8,128)} %analysis.1), calls=%async_computation | async-start | bytes 3145728 | tf_op jit(solution)/shard_map/all_to_all | solution.py:385
  17.4 0.0 copy-start.4
  17.5 0.0 copy-start.5
  18.8 38.4 %all-to-all-done.r_ref = f32[64,6,8,128]{3,2,1,0:T(8,128)S(1)} async-done(((f32[64,6,8,128]{3,2,1,0:T(8,128)}), f32[64,6,8,128]{3,2,1,0:T(8,128)S(1)}, u32[]{:S(2)}, u32[]{:S(2)}) %all-to-all-start) | async-done | bytes 1572896 | tf_op jit(solution)/shard_map/all_to_all | solution.py:385
  57.2 0.0 copy-done.1
  57.2 0.0 copy-done.2
  57.2 0.0 copy-done.3
  57.2 1.8 %forward.1 = (f32[1024,256]{1,0:T(8,128)S(1)}, f32[8,256]{1,0:T(8,128)S(1)}) custom-call(s32[1,2,8]{2,1,0:T(2,128)S(1)} %copy-done.3, s32[1]{0:T(128)S(6)} %copy.11.plane_ref, f32[64,6,8,128]{3,2,1,0:T(8,128)S(1)} %all-to-all-done.r_ref, f32[2,8,512]{2,1,0:T(8,128)S(1)} %copy-done.2, f32[4,2,16,512]{3,2,1,0:T(8,128)S(1)} %copy-done.1), custom_call_target="tpu_custom_call" | custom-call | tf_op jit(solution)/shard_map/forward/pallas_call | solution.py:387
  59.0 1.3 %collective-permute-start = (f32[8,256]{1,0:T(8,128)S(1)}, f32[8,256]{1,0:T(8,128)S(1)}, u32[]{:S(2)}, u32[]{:S(2)}) collective-permute-start(f32[8,256]{1,0:T(8,128)S(1)} %get-tuple-element.12), channel_id=1, source_target_pairs={{192,0},{0,64},{64,128},{128,192},{193,1},{1,65},{65,129},{129,193... | collective-permute-start | bytes 24584 | tf_op jit(solution)/shard_map/ppermute | solution.py:398
  60.3 0.0 copy-done.4
  60.3 0.0 copy-done.5
  60.3 2.4 %inverse.1 = (f32[64,6,8,128]{3,2,1,0:T(8,128)S(1)}, f32[64,6,8,128]{3,2,1,0:T(8,128)S(1)}) custom-call(s32[1]{0:T(128)S(6)} %copy.12.bound_ref, f32[1024,256]{1,0:T(8,128)S(1)} %get-tuple-element.9.c_ref, f32[4,2,32,128]{3,2,1,0:T(8,128)S(1)} %copy-done.4, f32[4,2,16,128]{3,2,1,0:T(8,128)S(1)} %copy-done.5), custom_call_target="tpu_custom_call" | custom-call | flops 1073741824 | bytes 4194304 | tf_op jit(solution)/shard_map/inverse/pallas_call | solution.py:399
  62.7 0.1 collective-permute-done.p_ref
  62.8 0.4 blend.1
  63.3 0.0 copy-start
  63.3 46.9 %all_to_all.10.q_ref = f32[64,6,8,128]{3,2,1,0:T(8,128)S(1)} all-to-all(f32[64,6,8,128]{3,2,1,0:T(8,128)S(1)} %blend.1), channel_id=1, replica_groups=mesh['ens'=4,'slab_0'=4,'slab_1'=8,'slab_2'=2] {'slab_0','slab_1','slab_2'}, dimensions={0} | all-to-all | bytes 3145728 | tf_op jit(solution)/shard_map/all_to_all | solution.py:417
  110.2 0.0 copy-done
  110.2 2.3 %synthesis.1 = f32[24,32,1024]{2,1,0:T(8,128)} custom-call(f32[64,6,8,128]{3,2,1,0:T(8,128)S(1)} %all_to_all.10.q_ref, bf16[2,2,256,512]{3,2,1,0:T(8,128)(2,1)S(1)} %copy-done), custom_call_target="tpu_custom_call" | custom-call | tf_op jit(solution)/shard_map/synthesis/pallas_call | solution.py:418
Async XLA Ops:
  4.1 53.1 %copy-start.1 = (f32[4,2,16,512]{3,2,1,0:T(8,128)S(1)}, f32[4,2,16,512]{3,2,1,0:T(8,128)}, u32[]{:S(2)}) copy-start(f32[4,2,16,512]{3,2,1,0:T(8,128)} %constant.14.clone.fi_ref) | copy-start | bytes 786436
  4.1 53.1 %copy-start.2 = (f32[2,8,512]{2,1,0:T(8,128)S(1)}, f32[2,8,512]{2,1,0:T(8,128)}, u32[]{:S(2)}) copy-start(f32[2,8,512]{2,1,0:T(8,128)} %constant.13.clone.ca_ref) | copy-start | bytes 98308
  4.1 53.1 %copy-start.3 = (s32[1,2,8]{2,1,0:T(2,128)S(1)}, s32[1,2,8]{2,1,0:T(2,128)}, u32[]{:S(2)}) copy-start(s32[1,2,8]{2,1,0:T(2,128)} %cut_ref.1) | copy-start | bytes 196
  4.1 53.1 %all-to-all-start = ((f32[64,6,8,128]{3,2,1,0:T(8,128)}), f32[64,6,8,128]{3,2,1,0:T(8,128)S(1)}, u32[]{:S(2)}, u32[]{:S(2)}) async-start(f32[64,6,8,128]{3,2,1,0:T(8,128)} %analysis.1), calls=%async_computation | async-start | bytes 3145728 | tf_op jit(solution)/shard_map/all_to_all | solution.py:385
  17.4 42.9 %copy-start.4 = (f32[4,2,32,128]{3,2,1,0:T(8,128)S(1)}, f32[4,2,32,128]{3,2,1,0:T(8,128)}, u32[]{:S(2)}) copy-start(f32[4,2,32,128]{3,2,1,0:T(8,128)} %constant.15.clone.fa_ref) | copy-start | bytes 393220
  17.5 42.9 %copy-start.5 = (f32[4,2,16,128]{3,2,1,0:T(8,128)S(1)}, f32[4,2,16,128]{3,2,1,0:T(8,128)}, u32[]{:S(2)}) copy-start(f32[4,2,16,128]{3,2,1,0:T(8,128)} %constant.16.clone.ne_ref) | copy-start | bytes 196612
  59.0 3.8 %collective-permute-start = (f32[8,256]{1,0:T(8,128)S(1)}, f32[8,256]{1,0:T(8,128)S(1)}, u32[]{:S(2)}, u32[]{:S(2)}) collective-permute-start(f32[8,256]{1,0:T(8,128)S(1)} %get-tuple-element.12), channel_id=1, source_target_pairs={{192,0},{0,64},{64,128},{128,192},{193,1},{1,65},{65,129},{129,193... | collective-permute-start | bytes 24584 | tf_op jit(solution)/shard_map/ppermute | solution.py:398
  63.3 46.9 %copy-start = (bf16[2,2,256,512]{3,2,1,0:T(8,128)(2,1)S(1)}, bf16[2,2,256,512]{3,2,1,0:T(8,128)(2,1)}, u32[]{:S(2)}) copy-start(bf16[2,2,256,512]{3,2,1,0:T(8,128)(2,1)} %constant.17.clone.table_ref) | copy-start | bytes 3145732
